TPU v7x, 128 devices: a whole 4x4x4 slice. The times are simulated.
128 devices in a mesh: dp: 4 (over z), expert: 16 (over y, x_hi, core), tensor: 2 (over x_lo).
Axes of the slice: x: 4 (x_hi: 2, x_lo: 2; x = x_hi * 2 + x_lo), y: 4, z: 4, core: 2. Of those that a mesh axis runs over, the one named last changes fastest.
Arguments:
- hidden: bfloat16 [8192, 6144], P(('dp', 'expert'), 'tensor'), may hold values from -6 to 6
- expert_ids: int32 [8192, 8], P(('dp', 'expert')), may hold values from 0 to 383, as said below
- gate_fixed: int32 [8192, 8], P(('dp', 'expert')), may hold values from 4096 to 65535
- slot_expert: int32 [64], replicated, may hold values from 0 to 383, as said below
- expert_in: bfloat16 [64, 6144, 2, 1024], P(('dp', 'expert'), 'tensor'), may hold values from -1 to 1, as said below
- expert_out: bfloat16 [64, 1024, 6144], P(('dp', 'expert'), None, 'tensor'), may hold values from -1 to 1, as said below
- shared_in: bfloat16 [6144, 2, 1024], P('tensor', None, 'dp'), may hold values from -0.078125 to 0.078125
- shared_out: bfloat16 [1024, 6144], P('dp', 'tensor'), may hold values from -0.1875 to 0.1875
Outputs:
- mixed: bfloat16 [8192, 6144], P(('dp', 'expert'), 'tensor')
Inputs may be any that keep to these rules, and one draw needn't show every extreme that they name: `expert_ids`: each row names 8 different experts. `slot_expert`: 56 different experts fill the 64 slots; 8 of them hold two slots each, the others one. `expert_in`: slots that hold the same expert hold the same weights. `expert_out`: slots that hold the same expert hold the same weights.
All inputs are finite; a program needn't handle non-finite values.
Results may differ from a plain program's by a relative error of at most 0.006.
Values may be sent and summed in bfloat16 or wider, within the bound.
No kernel may reach another device: no remote copies, remote signals or barrier semaphores. Data moves between devices by JAX's collectives and lax.ppermute only.
A program may use at most 192 MiB of HBM per device.

v0:
```python
import jax
import jax.numpy as jnp
from jax import lax
from jax.sharding import PartitionSpec as P

EXPERTS = 384
CAP = 4
gate_scale = 1.0 / 65536.0


def in_blocks(array, dim, devices):
    before, after = (array.shape[:dim], array.shape[dim + 1 :])
    return jnp.moveaxis(array.reshape(*before, devices, -1, *after), dim, 0)


def summed_on_arrival(array, axis, dim):
    parts = in_blocks(array, dim, lax.axis_size(axis))
    arrived = lax.all_to_all(parts, axis, split_axis=0, concat_axis=0, tiled=True)
    return arrived.astype(jnp.float32).sum(axis=0)


def swiglu(pre):
    return (jax.nn.silu(pre[:, 0, :]) * pre[:, 1, :]).astype(jnp.bfloat16)


def route_plan(chosen, row_rank, slot_expert):
    slot_count = slot_expert.shape[0]
    slot_iota = jnp.arange(slot_count, dtype=jnp.int32)[:, None]
    owns = slot_expert[:, None] == jnp.arange(chosen.shape[2], dtype=jnp.int32)[None, :]
    home = jnp.min(jnp.where(owns, slot_iota, slot_count), axis=0)
    spare = jnp.min(jnp.where(owns & (slot_iota != home[None, :]), slot_iota, slot_count), axis=0)
    home_of = jnp.sum(jnp.where(chosen, home[None, None, :], 0), axis=2)
    spare_of = jnp.sum(jnp.where(chosen, spare[None, None, :], 0), axis=2)
    first = row_rank < CAP
    spill = (row_rank >= CAP) & (row_rank < 2 * CAP) & (spare_of < slot_count)
    target = jnp.where(first, home_of, jnp.where(spill, spare_of, slot_count))
    slot_row = jnp.where(first, row_rank, row_rank - CAP)
    return (target, slot_row)


def dispatch_rows(send_rows):
    return lax.all_to_all(send_rows, ("dp", "expert"), split_axis=0, concat_axis=0, tiled=True)


def return_rows(answers):
    return lax.all_to_all(answers, ("dp", "expert"), split_axis=0, concat_axis=0, tiled=True)


def shards(
    hidden, expert_ids, gate_fixed, slot_expert, expert_in, expert_out, shared_in, shared_out
):
    tok_rows, half_width = hidden.shape
    topk_count = expert_ids.shape[1]
    slot_count = slot_expert.shape[0]
    experts_iota = jnp.arange(EXPERTS, dtype=jnp.int32)
    chosen = expert_ids[:, :, None] == experts_iota[None, None, :]
    picked = jnp.any(chosen, axis=1).astype(jnp.bfloat16)
    token_iota = jnp.arange(tok_rows, dtype=jnp.int32)
    earlier = (token_iota[:, None] > token_iota[None, :]).astype(jnp.bfloat16)
    before = jnp.dot(earlier, picked, preferred_element_type=jnp.float32)
    row_rank = jnp.sum(jnp.where(chosen, before[:, None, :], 0.0), axis=2).astype(jnp.int32)
    target, slot_row = route_plan(chosen, row_rank, slot_expert)
    flat_row = jnp.where(target < slot_count, target * CAP + slot_row, -1)
    row_iota = jnp.arange(slot_count * CAP, dtype=jnp.int32)
    owner = jnp.repeat(token_iota, topk_count)
    match_rows = flat_row.reshape(-1)[:, None] == row_iota[None, :]
    source_token = jnp.max(jnp.where(match_rows, owner[:, None], -1), axis=0)
    fetched_rows = jnp.take(hidden, jnp.maximum(source_token, 0), axis=0)
    send_rows = jnp.where(source_token[:, None] >= 0, fetched_rows, jnp.zeros((), jnp.bfloat16))
    piece = lax.all_gather(hidden, "dp", axis=0, tiled=True)
    partial_value = jnp.dot(
        piece, shared_in.reshape(half_width, -1), preferred_element_type=jnp.float32
    )
    shared_partial = partial_value.reshape(piece.shape[0], 2, -1)
    arrived = dispatch_rows(send_rows.reshape(slot_count, CAP, half_width))
    rows = arrived.reshape(-1, half_width)
    partial_value = jnp.dot(
        rows, expert_in[0].reshape(half_width, -1), preferred_element_type=jnp.float32
    )
    routed_partial = partial_value.reshape(rows.shape[0], 2, -1)
    shared_half, routed_half = (
        lax.psum_scatter(shared_partial, "tensor", scatter_dimension=2, tiled=True),
        lax.psum_scatter(routed_partial, "tensor", scatter_dimension=2, tiled=True),
    )
    shared_act, routed_act = (
        lax.all_gather(swiglu(shared_half), "tensor", axis=1, tiled=True),
        lax.all_gather(swiglu(routed_half), "tensor", axis=1, tiled=True),
    )
    shared_part = summed_on_arrival(
        jnp.dot(shared_act, shared_out, preferred_element_type=jnp.float32).astype(jnp.bfloat16),
        "dp",
        0,
    )
    answers = jnp.dot(routed_act, expert_out[0], preferred_element_type=jnp.float32).astype(
        jnp.bfloat16
    )
    returned = return_rows(answers.reshape(slot_count, CAP, half_width))
    returned = returned.reshape(-1, half_width)
    gates = gate_fixed.astype(jnp.float32) * gate_scale
    routed = jnp.zeros((tok_rows, half_width), jnp.float32)
    for column in range(topk_count):
        index = flat_row[:, column]
        answer_rows = jnp.take(returned, jnp.maximum(index, 0), axis=0).astype(jnp.float32)
        routed = routed + jnp.where(
            index[:, None] >= 0, gates[:, column : column + 1] * answer_rows, 0.0
        )
    return (shared_part + routed).astype(jnp.bfloat16)


def solution(mesh):
    in_specs = (
        P(("dp", "expert"), "tensor"),
        P(("dp", "expert"), None),
        P(("dp", "expert"), None),
        P(),
        P(("dp", "expert"), "tensor", None, None),
        P(("dp", "expert"), None, "tensor"),
        P("tensor", None, "dp"),
        P("dp", "tensor"),
    )
    out_specs = P(("dp", "expert"), "tensor")
    return jax.shard_map(shards, mesh=mesh, in_specs=in_specs, out_specs=out_specs, check_vma=False)
```

profile of v0, /device:TPU:1, one launch (start us, length us, event | category | flops | bytes accessed | tf_op | source)
XLA Modules:
  0.0 226.1 jit_solution(16265131079100112803)
XLA Ops:
  10.4 4.8 %select_reduce_fusion = (s32[128,8]{1,0:T(8,128)S(1)}, s32[128,8]{1,0:T(8,128)S(1)}) fusion(s32[384]{0:T(512)S(1)} %select_reduce_fusion.4, s32[128,8]{1,0:T(8,128)S(1)} %copy.22, s32[384]{0:T(512)S(1)} %select_reduce_fusion.5), kind=kLoop, calls=%fused_computation.18 | loop fusion | flops 1964032 | bytes 15360 | tf_op jit(solution)/shard_map/reduce_sum | solution.py:33
  17.3 2.7 %gather_fusion = bf16[256,3072]{1,0:T(8,128)(2,1)} fusion(bf16[128,3072]{1,0:T(8,128)(2,1)S(1)} %copy-done.1, s32[1024]{0:T(1024)S(1)} %pad_clamp_fusion.8), kind=kCustom, calls=%fused_computation.8 | custom fusion | bytes 3146752 | tf_op jit(solution)/shard_map/jit(_take)/gather | solution.py:68
  20.0 2.9 %gather.10 = bf16[64,4,3072]{2,1,0:T(4,128)(2,1)S(1)} reshape(bf16[256,3072]{1,0:T(8,128)(2,1)} %gather_fusion) | data formatting | bytes 3145728 | tf_op jit(solution)/shard_map/jit(_take)/gather | solution.py:68
  23.0 2.4 %select_select_fusion = bf16[64,4,3072]{2,1,0:T(4,128)(2,1)} fusion(bf16[64,4,3072]{2,1,0:T(4,128)(2,1)S(1)} %gather.10, pred[64,4]{1,0:T(8,128)(4,1)S(1)} %le.24, pred[64,4]{1,0:T(8,128)(4,1)S(1)} %ge.64), kind=kLoop, calls=%fused_computation.17 | loop fusion | flops 1572864 | bytes 3146240 | tf_op jit(solution)/shard_map/jit(_where)/select_n | solution.py:69
  25.4 12.5 %all-to-all-start.1 = ((bf16[64,4,3072]{2,1,0:T(4,128)(2,1)}), bf16[64,4,3072]{2,1,0:T(4,128)(2,1)S(1)}, u32[]{:S(2)}, u32[]{:S(2)}) async-start(bf16[64,4,3072]{2,1,0:T(4,128)(2,1)} %select_select_fusion), calls=%async_computation.2 | async-start | bytes 3145728 | tf_op jit(solution)/shard_map/all_to_all | solution.py:42
  38.1 13.1 %copy.25 = bf16[384,8,2,1024]{3,1,2,0:T(8,128)(2,1)} copy(bf16[384,8,2,1024]{3,2,1,0:T(2,128)(2,1)} %bitcast.65) | data formatting | bytes 25165824
  51.2 16.6 %copy.23 = bf16[2048,3072]{1,0:T(8,128)(2,1)} copy(bf16[2048,3072]{0,1:T(8,128)(2,1)} %bitcast.63) | data formatting | bytes 25165824 | tf_op jit(solution)/shard_map/dot_general | solution.py:77
  69.2 9.9 %fusion.18 = f32[256,2,1024]{2,0,1:T(8,128)} fusion(bf16[256,3072,1]{1,0,2:T(8,128)(2,1)} %reshape.218, bf16[2,1024,3072]{2,1,0:T(8,128)(2,1)} %bitcast.66), kind=kOutput, calls=%fused_computation.101 | convolution fusion | flops 3221225472 | bytes 16252928 | tf_op jit(solution)/shard_map/dot_general | solution.py:77
  79.2 4.1 %copy.24 = bf16[384,8,2,256]{3,1,2,0:T(8,128)(2,1)} copy(bf16[384,8,2,256]{3,2,1,0:T(2,128)(2,1)} %bitcast.68) | data formatting | bytes 6291456
  83.3 4.6 %copy.21 = bf16[512,3072]{1,0:T(8,128)(2,1)} copy(bf16[512,3072]{0,1:T(8,128)(2,1)} %bitcast.67) | data formatting | bytes 6291456 | tf_op jit(solution)/shard_map/dot_general | solution.py:71
  87.9 6.4 %fusion.5 = f32[512,2,256]{2,0,1:T(8,128)} fusion(bf16[2,256,3072]{2,1,0:T(8,128)(2,1)} %bitcast.69, bf16[512,3072]{1,0:T(8,128)(2,1)} %all-gather.2.cloned.1.call-done), kind=kOutput, calls=%fused_computation.14 | convolution fusion | flops 1610612736 | bytes 7340032 | tf_op jit(solution)/shard_map/dot_general | solution.py:71
  94.4 20.0 %reduce-scatter.5.cloned.1.call-done = f32[256,2,512]{2,0,1:T(8,128)} async-done(((f32[256,2,1024]{2,0,1:T(8,128)}), f32[256,2,512]{2,0,1:T(8,128)}) %reduce-scatter.5.cloned.1.call-update) | async-done | bytes 1048592 | tf_op jit(solution)/shard_map/reduce_scatter | solution.py:83
  115.8 7.6 %all_gather.11 = bf16[256,1024]{1,0:T(8,128)(2,1)S(1)} all-gather(bf16[256,512]{1,0:T(8,128)(2,1)S(1)} %fusion.9), channel_id=1, replica_groups=mesh['dp'=4,'expert'=16,'tensor'=2] {'tensor'}, dimensions={1}, use_global_device_ids=true | all-gather | bytes 786432 | tf_op jit(solution)/shard_map/all_gather | solution.py:87
  123.4 4.6 %fusion.2 = bf16[256,3072]{1,0:T(8,128)(2,1)S(1)} fusion(bf16[256,1024]{1,0:T(8,128)(2,1)S(1)} %all_gather.11, bf16[1,1024,3072]{2,1,0:T(8,128)(2,1)} %param.15), kind=kOutput, calls=%fused_computation.13 | convolution fusion | flops 1611399168 | bytes 8388608 | tf_op jit(solution)/shard_map/dot_general | solution.py:94
  129.4 11.5 %all-to-all-start.2 = ((bf16[64,4,3072]{2,1,0:T(4,128)(2,1)}), bf16[64,4,3072]{2,1,0:T(4,128)(2,1)S(1)}, u32[]{:S(2)}, u32[]{:S(2)}) async-start(bf16[64,4,3072]{2,1,0:T(4,128)(2,1)} %reshape.118), calls=%async_computation.4 | async-start | bytes 3145728 | tf_op jit(solution)/shard_map/all_to_all | solution.py:46
  142.5 18.5 %all_gather.10 = bf16[512,256]{1,0:T(8,128)(2,1)S(1)} all-gather(bf16[512,128]{1,0:T(8,128)(2,1)S(1)} %fusion.11), channel_id=1, replica_groups=mesh['dp'=4,'expert'=16,'tensor'=2] {'tensor'}, dimensions={1}, use_global_device_ids=true | all-gather | bytes 393216 | tf_op jit(solution)/shard_map/all_gather | solution.py:86
  161.0 2.7 %convolution_convert_fusion = bf16[512,3072]{1,0:T(8,128)(2,1)} fusion(bf16[512,256]{1,0:T(8,128)(2,1)S(1)} %all_gather.10, bf16[256,3072]{1,0:T(8,128)(2,1)S(1)} %copy-done), kind=kOutput, calls=%fused_computation.12 | convolution fusion | flops 806879232 | bytes 4980736 | tf_op jit(solution)/shard_map/dot_general | solution.py:90
  163.7 3.1 %all-to-all-done.2 = bf16[64,4,3072]{2,1,0:T(4,128)(2,1)S(1)} async-done(((bf16[64,4,3072]{2,1,0:T(4,128)(2,1)}), bf16[64,4,3072]{2,1,0:T(4,128)(2,1)S(1)}, u32[]{:S(2)}, u32[]{:S(2)}) %all-to-all-start.2) | async-done | bytes 1572896 | tf_op jit(solution)/shard_map/all_to_all | solution.py:46
  167.9 4.9 %all-to-all-start = ((bf16[4,128,3072]{2,1,0:T(8,128)(2,1)}), bf16[4,128,3072]{2,1,0:T(8,128)(2,1)}, u32[]{:S(2)}, u32[]{:S(2)}) async-start(bf16[4,128,3072]{2,1,0:T(8,128)(2,1)} %bitcast.64), calls=%async_computation.1 | async-start | bytes 6291456 | tf_op jit(solution)/shard_map/all_to_all | solution.py:18
  173.3 2.7 %reshape.119 = bf16[256,3072]{1,0:T(8,128)(2,1)S(1)} reshape(bf16[64,4,3072]{2,1,0:T(4,128)(2,1)} %copy-done.2) | data formatting | bytes 3145728 | tf_op jit(solution)/shard_map/reshape | solution.py:98
  179.9 2.0 gather_fusion.4
  191.6 18.4 %all-to-all-done = bf16[4,128,3072]{2,1,0:T(8,128)(2,1)} async-done(((bf16[4,128,3072]{2,1,0:T(8,128)(2,1)}), bf16[4,128,3072]{2,1,0:T(8,128)(2,1)}, u32[]{:S(2)}, u32[]{:S(2)}) %all-to-all-start) | async-done | bytes 3145760 | tf_op jit(solution)/shard_map/all_to_all | solution.py:18
  210.0 2.8 %convert_reduce_fusion = f32[128,3072]{1,0:T(8,128)S(1)} fusion(bf16[4,128,3072]{2,1,0:T(8,128)(2,1)} %all-to-all-done), kind=kLoop, calls=%fused_computation.11 | loop fusion | flops 2752512 | bytes 4718592 | tf_op jit(solution)/shard_map/reduce_sum | solution.py:19
  212.8 5.9 %add_convert_fusion = bf16[128,3072]{1,0:T(8,128)(2,1)} fusion(f32[128,3072]{1,0:T(8,128)S(1)} %convert_reduce_fusion, bf16[128,3072]{1,0:T(8,128)(2,1)} %gather_fusion.8, bf16[128,3072]{1,0:T(8,128)(2,1)S(1)} %copy-done.8, bf16[128,3072]{1,0:T(8,128)(2,1)S(1)} %copy-done.7, bf16[128,3072]{1,0:T(8,128)(2,1)S(1)} %copy-done.6, ...), kind=kLoop, calls=%fused_computation.16 | loop fusion | flops 16121856 | bytes 8656896 | tf_op jit(solution)/shard_map/convert_element_type | solution.py:107
  (80 shorter events, 26.3 us)
Async XLA Ops:
  7.4 153.6 %copy-start = (bf16[256,3072]{1,0:T(8,128)(2,1)S(1)}, bf16[256,3072]{1,0:T(8,128)(2,1)}, u32[]{:S(2)}) copy-start(bf16[256,3072]{1,0:T(8,128)(2,1)} %param.17) | copy-start | bytes 4718596
  7.4 9.9 %copy-start.1 = (bf16[128,3072]{1,0:T(8,128)(2,1)S(1)}, bf16[128,3072]{1,0:T(8,128)(2,1)}, u32[]{:S(2)}) copy-start(bf16[128,3072]{1,0:T(8,128)(2,1)} %param.10) | copy-start | bytes 2359300
  7.4 80.6 %all-gather.2.cloned.1.call-start = ((), (), s32[]{:S(2)}) async-start(), calls=%async_computation.5 | async-start | bytes 3932160 | tf_op jit(solution)/shard_map/all_gather | solution.py:70
  25.4 42.5 %all-to-all-start.1 = ((bf16[64,4,3072]{2,1,0:T(4,128)(2,1)}), bf16[64,4,3072]{2,1,0:T(4,128)(2,1)S(1)}, u32[]{:S(2)}, u32[]{:S(2)}) async-start(bf16[64,4,3072]{2,1,0:T(4,128)(2,1)} %select_select_fusion), calls=%async_computation.2 | async-start | bytes 3145728 | tf_op jit(solution)/shard_map/all_to_all | solution.py:42
  37.9 76.5 %reduce-scatter.5.cloned.1.call-start = ((), (), s32[]{:S(2)}) async-start(), calls=%async_computation.7 | async-start | bytes 3145728 | tf_op jit(solution)/shard_map/reduce_scatter | solution.py:83
  79.1 62.3 %reduce-scatter.3.cloned.1.call-start = ((), (), s32[]{:S(2)}) async-start(), calls=%async_computation.6 | async-start | bytes 1572864 | tf_op jit(solution)/shard_map/reduce_scatter | solution.py:82
  129.4 37.3 %all-to-all-start.2 = ((bf16[64,4,3072]{2,1,0:T(4,128)(2,1)}), bf16[64,4,3072]{2,1,0:T(4,128)(2,1)S(1)}, u32[]{:S(2)}, u32[]{:S(2)}) async-start(bf16[64,4,3072]{2,1,0:T(4,128)(2,1)} %reshape.118), calls=%async_computation.4 | async-start | bytes 3145728 | tf_op jit(solution)/shard_map/all_to_all | solution.py:46
  166.7 1.1 copy-start.2
  166.7 6.5 %copy-start.9 = (s32[128,8]{0,1:T(8,128)S(1)}, s32[128,8]{0,1:T(8,128)}, u32[]{:S(2)}) copy-start(s32[128,8]{0,1:T(8,128)} %param.12) | copy-start | bytes 12292
  167.9 42.1 %all-to-all-start = ((bf16[4,128,3072]{2,1,0:T(8,128)(2,1)}), bf16[4,128,3072]{2,1,0:T(8,128)(2,1)}, u32[]{:S(2)}, u32[]{:S(2)}) async-start(bf16[4,128,3072]{2,1,0:T(8,128)(2,1)} %bitcast.64), calls=%async_computation.1 | async-start | bytes 6291456 | tf_op jit(solution)/shard_map/all_to_all | solution.py:18
  191.6 21.2 %copy-start.3 = (bf16[128,3072]{1,0:T(8,128)(2,1)S(1)}, bf16[128,3072]{1,0:T(8,128)(2,1)}, u32[]{:S(2)}) copy-start(bf16[128,3072]{1,0:T(8,128)(2,1)} %gather_fusion.2) | copy-start | bytes 2359300
  191.6 21.2 %copy-start.4 = (bf16[128,3072]{1,0:T(8,128)(2,1)S(1)}, bf16[128,3072]{1,0:T(8,128)(2,1)}, u32[]{:S(2)}) copy-start(bf16[128,3072]{1,0:T(8,128)(2,1)} %gather_fusion.3) | copy-start | bytes 2359300
  210.0 2.8 %copy-start.5 = (bf16[128,3072]{1,0:T(8,128)(2,1)S(1)}, bf16[128,3072]{1,0:T(8,128)(2,1)}, u32[]{:S(2)}) copy-start(bf16[128,3072]{1,0:T(8,128)(2,1)} %gather_fusion.4) | copy-start | bytes 2359300
  210.0 2.8 %copy-start.6 = (bf16[128,3072]{1,0:T(8,128)(2,1)S(1)}, bf16[128,3072]{1,0:T(8,128)(2,1)}, u32[]{:S(2)}) copy-start(bf16[128,3072]{1,0:T(8,128)(2,1)} %gather_fusion.5) | copy-start | bytes 2359300
  210.0 2.8 %copy-start.7 = (bf16[128,3072]{1,0:T(8,128)(2,1)S(1)}, bf16[128,3072]{1,0:T(8,128)(2,1)}, u32[]{:S(2)}) copy-start(bf16[128,3072]{1,0:T(8,128)(2,1)} %gather_fusion.6) | copy-start | bytes 2359300
  210.0 2.9 %copy-start.8 = (bf16[128,3072]{1,0:T(8,128)(2,1)S(1)}, bf16[128,3072]{1,0:T(8,128)(2,1)}, u32[]{:S(2)}) copy-start(bf16[128,3072]{1,0:T(8,128)(2,1)} %gather_fusion.7) | copy-start | bytes 2359300
Sparse Core Ops, SparseCore 0:
  9.8 59.5 all-gather.1
Sparse Core Ops, SparseCore 1:
  79.2 35.1 reduce-scatter.4
  116.6 23.8 reduce-scatter.2
where the time goes:
time: 227 us; the launch traced here: 226 us
  local copies, waits for them, and re-layouts  67.8 us (30%)
  waiting for transfers between devices  42.2 us (19%)
  starting transfers between devices  29.1 us (13%)
  blocking collectives  26.1 us (11%)
  matrix products  23.7 us (10%)
  other arithmetic  22 us (10%)
  between operations  15.2 us (7%)
    reduce_scatter x1, waiting for transfers between devices, shards(): lax.psum_scatter(routed_partial, 'tensor', scatter_dimension=2, tiled=True)  20 us
    unnamed x23, local copies, waits for them, and re-layouts  19.2 us
    all_gather x1, blocking collectives, shards(): lax.all_gather(swiglu(shared_half), 'tensor', axis=1, tiled=True)  18.5 us
    all_to_all x1, waiting for transfers between devices, summed_on_arrival(): lax.all_to_all(parts, axis, split_axis=0, concat_axis=0, tiled=True)  18.4 us
    dot_general x1, local copies, waits for them, and re-layouts, shards(): jnp.dot(rows, expert_in[0].reshape(half_width, -1), preferred_element_typ...  16.6 us
    gather x8, local copies, waits for them, and re-layouts, shards(): jnp.take(returned, jnp.maximum(index, 0), axis=0).astype(jnp.float32)  15.5 us
    all_to_all x1, starting transfers between devices, dispatch_rows(): lax.all_to_all(send_rows, ('dp', 'expert'), split_axis=0, concat_axis=0,...  12.5 us
    all_to_all x1, starting transfers between devices, return_rows(): lax.all_to_all(answers, ('dp', 'expert'), split_axis=0, concat_axis=0, ti...  11.5 us
  transfers between devices with their start and end apart: 6, of which 3 were waited for; matrix products, arithmetic and copies ran while one was open for 46% of the time, Pallas kernels for 0%

commit v1 on v0

--- a/solution.py
+++ b/solution.py
@@ -83,7 +83,12 @@
         lax.psum_scatter(routed_partial, "tensor", scatter_dimension=2, tiled=True),
     )
     shared_act, routed_act = (
-        lax.all_gather(swiglu(shared_half), "tensor", axis=1, tiled=True),
+        jnp.concatenate(
+            lax.all_to_all(
+                jnp.stack([swiglu(shared_half)] * lax.axis_size("tensor")), "tensor", 0, 0
+            ),
+            axis=1,
+        ),
         lax.all_gather(swiglu(routed_half), "tensor", axis=1, tiled=True),
     )
     shared_part = summed_on_arrival(

time: 227 us -> 249 us (1.097)
  waiting for transfers between devices: 42.2 us -> 76.3 us
  blocking collectives: 26.1 us -> 7.73 us
    all_gather x1 -> x0, blocking collectives: 18.5 us -> none  [shards(): lax.all_gather(swiglu(shared_half), 'tensor', axis=1, tiled=True)]
    all_to_all x1, waiting for transfers between devices: 3.06 us -> 20.3 us  [return_rows(): lax.all_to_all(answers, ('dp', 'expert'), split_axis=0, concat_axis=0, ti...]
    reduce_scatter x1, waiting for transfers between devices: 0.03 us -> 17 us  [shards(): lax.psum_scatter(shared_partial, 'tensor', scatter_dimension=2, tiled=True)]
    all_to_all x0 -> x1, starting transfers between devices: none -> 3.44 us  [shards(): lax.all_to_all(jnp.stack([swiglu(shared_half)] * lax.axis_size('tensor'))...]
    unnamed x23 -> x29, local copies, waits for them, and re-layouts: 19.2 us -> 19.9 us
  transfers between devices with their start and end apart: 6 -> 7, of which waited for: 3 -> 4; matrix products, arithmetic and copies ran while one was open for 46% -> 42% of each run, Pallas kernels for 0% -> 0%
where the time goes in v1:
time: 249 us; the launch traced here: 248 us
  waiting for transfers between devices  76.3 us (31%)
  local copies, waits for them, and re-layouts  69.6 us (28%)
  starting transfers between devices  31.5 us (13%)
  matrix products  23.8 us (10%)
  other arithmetic  23.6 us (9%)
  between operations  15.3 us (6%)
  blocking collectives  7.73 us (3%)
    all_to_all x1, waiting for transfers between devices, return_rows(): lax.all_to_all(answers, ('dp', 'expert'), split_axis=0, concat_axis=0, ti...  20.3 us
    reduce_scatter x1, waiting for transfers between devices, shards(): lax.psum_scatter(routed_partial, 'tensor', scatter_dimension=2, tiled=True)  20.1 us
    unnamed x29, local copies, waits for them, and re-layouts  19.9 us
    all_to_all x1, waiting for transfers between devices, summed_on_arrival(): lax.all_to_all(parts, axis, split_axis=0, concat_axis=0, tiled=True)  18.1 us
    reduce_scatter x1, waiting for transfers between devices, shards(): lax.psum_scatter(shared_partial, 'tensor', scatter_dimension=2, tiled=True)  17 us
    dot_general x1, local copies, waits for them, and re-layouts, shards(): jnp.dot(rows, expert_in[0].reshape(half_width, -1), preferred_element_typ...  16.6 us
    gather x8, local copies, waits for them, and re-layouts, shards(): jnp.take(returned, jnp.maximum(index, 0), axis=0).astype(jnp.float32)  15.5 us
    all_to_all x1, starting transfers between devices, dispatch_rows(): lax.all_to_all(send_rows, ('dp', 'expert'), split_axis=0, concat_axis=0,...  12.5 us
  transfers between devices with their start and end apart: 7, of which 4 were waited for; matrix products, arithmetic and copies ran while one was open for 42% of the time, Pallas kernels for 0%

profile of v1, /device:TPU:1, one launch (start us, length us, event | category | flops | bytes accessed | tf_op | source)
XLA Modules:
  0.0 247.9 jit_solution(6258748380258505941)
XLA Ops:
  10.4 4.8 %select_reduce_fusion = (s32[128,8]{1,0:T(8,128)S(1)}, s32[128,8]{1,0:T(8,128)S(1)}) fusion(s32[384]{0:T(512)S(1)} %select_reduce_fusion.4, s32[128,8]{1,0:T(8,128)S(1)} %copy.25, s32[384]{0:T(512)S(1)} %select_reduce_fusion.5), kind=kLoop, calls=%fused_computation.18 | loop fusion | flops 1964032 | bytes 15360 | tf_op jit(solution)/shard_map/reduce_sum | solution.py:33
  17.4 2.7 %gather_fusion = bf16[256,3072]{1,0:T(8,128)(2,1)} fusion(bf16[128,3072]{1,0:T(8,128)(2,1)S(1)} %copy-done.1, s32[1024]{0:T(1024)S(1)} %pad_clamp_fusion.8), kind=kCustom, calls=%fused_computation.8 | custom fusion | bytes 3146752 | tf_op jit(solution)/shard_map/jit(_take)/gather | solution.py:68
  20.1 2.9 %gather.10 = bf16[64,4,3072]{2,1,0:T(4,128)(2,1)S(1)} reshape(bf16[256,3072]{1,0:T(8,128)(2,1)} %gather_fusion) | data formatting | bytes 3145728 | tf_op jit(solution)/shard_map/jit(_take)/gather | solution.py:68
  23.0 2.4 select_select_fusion
  25.4 12.5 %all-to-all-start.2 = ((bf16[64,4,3072]{2,1,0:T(4,128)(2,1)}), bf16[64,4,3072]{2,1,0:T(4,128)(2,1)S(1)}, u32[]{:S(2)}, u32[]{:S(2)}) async-start(bf16[64,4,3072]{2,1,0:T(4,128)(2,1)} %select_select_fusion), calls=%async_computation.3 | async-start | bytes 3145728 | tf_op jit(solution)/shard_map/all_to_all | solution.py:42
  38.2 13.1 %copy.28 = bf16[384,8,2,1024]{3,1,2,0:T(8,128)(2,1)} copy(bf16[384,8,2,1024]{3,2,1,0:T(2,128)(2,1)} %bitcast.67) | data formatting | bytes 25165824
  51.3 16.6 %copy.26 = bf16[2048,3072]{1,0:T(8,128)(2,1)} copy(bf16[2048,3072]{0,1:T(8,128)(2,1)} %bitcast.65) | data formatting | bytes 25165824 | tf_op jit(solution)/shard_map/dot_general | solution.py:77
  69.3 9.9 %fusion.18 = f32[256,2,1024]{2,0,1:T(8,128)} fusion(bf16[256,3072,1]{1,0,2:T(8,128)(2,1)} %reshape.267, bf16[2,1024,3072]{2,1,0:T(8,128)(2,1)} %bitcast.68), kind=kOutput, calls=%fused_computation.102 | convolution fusion | flops 3221225472 | bytes 16252928 | tf_op jit(solution)/shard_map/dot_general | solution.py:77
  79.2 4.1 %copy.27 = bf16[384,8,2,256]{3,1,2,0:T(8,128)(2,1)} copy(bf16[384,8,2,256]{3,2,1,0:T(2,128)(2,1)} %bitcast.70) | data formatting | bytes 6291456
  83.3 4.6 %copy.23 = bf16[512,3072]{1,0:T(8,128)(2,1)} copy(bf16[512,3072]{0,1:T(8,128)(2,1)} %bitcast.69) | data formatting | bytes 6291456 | tf_op jit(solution)/shard_map/dot_general | solution.py:71
  88.0 6.3 %fusion.5 = f32[512,2,256]{2,0,1:T(8,128)} fusion(bf16[2,256,3072]{2,1,0:T(8,128)(2,1)} %bitcast.71, bf16[512,3072]{1,0:T(8,128)(2,1)} %all-gather.2.cloned.1.call-done), kind=kOutput, calls=%fused_computation.14 | convolution fusion | flops 1610612736 | bytes 7340032 | tf_op jit(solution)/shard_map/dot_general | solution.py:71
  94.3 20.1 %reduce-scatter.5.cloned.1.call-done = f32[256,2,512]{2,0,1:T(8,128)} async-done(((f32[256,2,1024]{2,0,1:T(8,128)}), f32[256,2,512]{2,0,1:T(8,128)}) %reduce-scatter.5.cloned.1.call-update) | async-done | bytes 1048592 | tf_op jit(solution)/shard_map/reduce_scatter | solution.py:83
  115.8 7.7 %all_gather.7 = bf16[256,1024]{1,0:T(8,128)(2,1)} all-gather(bf16[256,512]{1,0:T(8,128)(2,1)S(1)} %fusion.9), channel_id=1, replica_groups=mesh['dp'=4,'expert'=16,'tensor'=2] {'tensor'}, dimensions={1}, use_global_device_ids=true | all-gather | bytes 786432 | tf_op jit(solution)/shard_map/all_gather | solution.py:92
  123.5 17.0 %reduce-scatter.3.cloned.1.call-done = f32[512,2,128]{2,0,1:T(8,128)} async-done(((f32[512,2,256]{2,0,1:T(8,128)}), f32[512,2,128]{2,0,1:T(8,128)}) %reduce-scatter.3.cloned.1.call-update) | async-done | bytes 524304 | tf_op jit(solution)/shard_map/reduce_scatter | solution.py:82
  142.3 3.4 %all-to-all-start = ((bf16[2,512,128]{2,1,0:T(8,128)(2,1)}), bf16[2,512,128]{2,1,0:T(8,128)(2,1)S(1)}, u32[]{:S(2)}, u32[]{:S(2)}) async-start(bf16[2,512,128]{2,1,0:T(8,128)(2,1)} %pad_maximum_fusion), calls=%async_computation.1 | async-start | bytes 524288 | tf_op jit(solution)/shard_map/all_to_all | solution.py:87
  145.8 4.8 %fusion.2 = bf16[256,3072]{1,0:T(8,128)(2,1)S(1)} fusion(bf16[256,1024]{1,0:T(8,128)(2,1)} %all_gather.7, bf16[1,1024,3072]{2,1,0:T(8,128)(2,1)} %param.15), kind=kOutput, calls=%fused_computation.13 | convolution fusion | flops 1611399168 | bytes 8388608 | tf_op jit(solution)/shard_map/dot_general | solution.py:99
  152.8 10.5 %all-to-all-start.3 = ((bf16[64,4,3072]{2,1,0:T(4,128)(2,1)}), bf16[64,4,3072]{2,1,0:T(4,128)(2,1)S(1)}, u32[]{:S(2)}, u32[]{:S(2)}) async-start(bf16[64,4,3072]{2,1,0:T(4,128)(2,1)} %reshape.167), calls=%async_computation.5 | async-start | bytes 3145728 | tf_op jit(solution)/shard_map/all_to_all | solution.py:46
  165.7 2.7 %convolution_convert_fusion = bf16[512,3072]{1,0:T(8,128)(2,1)} fusion(bf16[512,256]{0,1:T(8,128)(2,1)S(1)} %bitcast.72, bf16[256,3072]{1,0:T(8,128)(2,1)S(1)} %copy-done), kind=kOutput, calls=%fused_computation.12 | convolution fusion | flops 806879232 | bytes 4980736 | tf_op jit(solution)/shard_map/dot_general | solution.py:95
  168.3 20.3 %all-to-all-done.3 = bf16[64,4,3072]{2,1,0:T(4,128)(2,1)S(1)} async-done(((bf16[64,4,3072]{2,1,0:T(4,128)(2,1)}), bf16[64,4,3072]{2,1,0:T(4,128)(2,1)S(1)}, u32[]{:S(2)}, u32[]{:S(2)}) %all-to-all-start.3) | async-done | bytes 1572896 | tf_op jit(solution)/shard_map/all_to_all | solution.py:46
  189.8 4.9 %all-to-all-start.1 = ((bf16[4,128,3072]{2,1,0:T(8,128)(2,1)}), bf16[4,128,3072]{2,1,0:T(8,128)(2,1)}, u32[]{:S(2)}, u32[]{:S(2)}) async-start(bf16[4,128,3072]{2,1,0:T(8,128)(2,1)} %bitcast.66), calls=%async_computation.2 | async-start | bytes 6291456 | tf_op jit(solution)/shard_map/all_to_all | solution.py:18
  195.3 2.7 %reshape.168 = bf16[256,3072]{1,0:T(8,128)(2,1)S(1)} reshape(bf16[64,4,3072]{2,1,0:T(4,128)(2,1)} %copy-done.2) | data formatting | bytes 3145728 | tf_op jit(solution)/shard_map/reshape | solution.py:103
  213.6 18.1 %all-to-all-done.1 = bf16[4,128,3072]{2,1,0:T(8,128)(2,1)} async-done(((bf16[4,128,3072]{2,1,0:T(8,128)(2,1)}), bf16[4,128,3072]{2,1,0:T(8,128)(2,1)}, u32[]{:S(2)}, u32[]{:S(2)}) %all-to-all-start.1) | async-done | bytes 3145760 | tf_op jit(solution)/shard_map/all_to_all | solution.py:18
  231.7 2.8 %convert_reduce_fusion = f32[128,3072]{1,0:T(8,128)S(1)} fusion(bf16[4,128,3072]{2,1,0:T(8,128)(2,1)} %all-to-all-done.1), kind=kLoop, calls=%fused_computation.11 | loop fusion | flops 2752512 | bytes 4718592 | tf_op jit(solution)/shard_map/reduce_sum | solution.py:19
  234.6 5.9 %add_convert_fusion = bf16[128,3072]{1,0:T(8,128)(2,1)} fusion(f32[128,3072]{1,0:T(8,128)S(1)} %convert_reduce_fusion, bf16[128,3072]{1,0:T(8,128)(2,1)} %gather_fusion.8, bf16[128,3072]{1,0:T(8,128)(2,1)S(1)} %copy-done.8, bf16[128,3072]{1,0:T(8,128)(2,1)S(1)} %copy-done.7, bf16[128,3072]{1,0:T(8,128)(2,1)S(1)} %copy-done.6, ...), kind=kLoop, calls=%fused_computation.16 | loop fusion | flops 16121856 | bytes 8656896 | tf_op jit(solution)/shard_map/convert_element_type | solution.py:112
  (89 shorter events, 31.7 us)
Async XLA Ops:
  7.4 158.3 %copy-start = (bf16[256,3072]{1,0:T(8,128)(2,1)S(1)}, bf16[256,3072]{1,0:T(8,128)(2,1)}, u32[]{:S(2)}) copy-start(bf16[256,3072]{1,0:T(8,128)(2,1)} %param.17) | copy-start | bytes 4718596
  7.4 10.0 %copy-start.1 = (bf16[128,3072]{1,0:T(8,128)(2,1)S(1)}, bf16[128,3072]{1,0:T(8,128)(2,1)}, u32[]{:S(2)}) copy-start(bf16[128,3072]{1,0:T(8,128)(2,1)} %param.10) | copy-start | bytes 2359300
  7.4 80.6 %all-gather.2.cloned.1.call-start = ((), (), s32[]{:S(2)}) async-start(), calls=%async_computation.6 | async-start | bytes 3932160 | tf_op jit(solution)/shard_map/all_gather | solution.py:70
  15.2 2.2 copy-start.10
  16.5 0.9 copy-start.11
  25.4 42.5 %all-to-all-start.2 = ((bf16[64,4,3072]{2,1,0:T(4,128)(2,1)}), bf16[64,4,3072]{2,1,0:T(4,128)(2,1)S(1)}, u32[]{:S(2)}, u32[]{:S(2)}) async-start(bf16[64,4,3072]{2,1,0:T(4,128)(2,1)} %select_select_fusion), calls=%async_computation.3 | async-start | bytes 3145728 | tf_op jit(solution)/shard_map/all_to_all | solution.py:42
  37.9 76.5 %reduce-scatter.5.cloned.1.call-start = ((), (), s32[]{:S(2)}) async-start(), calls=%async_computation.8 | async-start | bytes 3145728 | tf_op jit(solution)/shard_map/reduce_scatter | solution.py:83
  79.2 61.4 %reduce-scatter.3.cloned.1.call-start = ((), (), s32[]{:S(2)}) async-start(), calls=%async_computation.7 | async-start | bytes 1572864 | tf_op jit(solution)/shard_map/reduce_scatter | solution.py:82
  142.3 9.7 %all-to-all-start = ((bf16[2,512,128]{2,1,0:T(8,128)(2,1)}), bf16[2,512,128]{2,1,0:T(8,128)(2,1)S(1)}, u32[]{:S(2)}, u32[]{:S(2)}) async-start(bf16[2,512,128]{2,1,0:T(8,128)(2,1)} %pad_maximum_fusion), calls=%async_computation.1 | async-start | bytes 524288 | tf_op jit(solution)/shard_map/all_to_all | solution.py:87
  152.0 0.7 copy-start.9
  152.8 35.9 %all-to-all-start.3 = ((bf16[64,4,3072]{2,1,0:T(4,128)(2,1)}), bf16[64,4,3072]{2,1,0:T(4,128)(2,1)S(1)}, u32[]{:S(2)}, u32[]{:S(2)}) async-start(bf16[64,4,3072]{2,1,0:T(4,128)(2,1)} %reshape.167), calls=%async_computation.5 | async-start | bytes 3145728 | tf_op jit(solution)/shard_map/all_to_all | solution.py:46
  188.7 1.1 copy-start.2
  188.7 6.5 %copy-start.12 = (s32[128,8]{0,1:T(8,128)S(1)}, s32[128,8]{0,1:T(8,128)}, u32[]{:S(2)}) copy-start(s32[128,8]{0,1:T(8,128)} %param.12) | copy-start | bytes 12292
  189.8 41.9 %all-to-all-start.1 = ((bf16[4,128,3072]{2,1,0:T(8,128)(2,1)}), bf16[4,128,3072]{2,1,0:T(8,128)(2,1)}, u32[]{:S(2)}, u32[]{:S(2)}) async-start(bf16[4,128,3072]{2,1,0:T(8,128)(2,1)} %bitcast.66), calls=%async_computation.2 | async-start | bytes 6291456 | tf_op jit(solution)/shard_map/all_to_all | solution.py:18
  213.6 20.9 %copy-start.3 = (bf16[128,3072]{1,0:T(8,128)(2,1)S(1)}, bf16[128,3072]{1,0:T(8,128)(2,1)}, u32[]{:S(2)}) copy-start(bf16[128,3072]{1,0:T(8,128)(2,1)} %gather_fusion.2) | copy-start | bytes 2359300
  213.6 20.9 %copy-start.4 = (bf16[128,3072]{1,0:T(8,128)(2,1)S(1)}, bf16[128,3072]{1,0:T(8,128)(2,1)}, u32[]{:S(2)}) copy-start(bf16[128,3072]{1,0:T(8,128)(2,1)} %gather_fusion.3) | copy-start | bytes 2359300
  231.7 2.8 %copy-start.5 = (bf16[128,3072]{1,0:T(8,128)(2,1)S(1)}, bf16[128,3072]{1,0:T(8,128)(2,1)}, u32[]{:S(2)}) copy-start(bf16[128,3072]{1,0:T(8,128)(2,1)} %gather_fusion.4) | copy-start | bytes 2359300
  231.7 2.8 %copy-start.6 = (bf16[128,3072]{1,0:T(8,128)(2,1)S(1)}, bf16[128,3072]{1,0:T(8,128)(2,1)}, u32[]{:S(2)}) copy-start(bf16[128,3072]{1,0:T(8,128)(2,1)} %gather_fusion.5) | copy-start | bytes 2359300
  231.7 2.8 %copy-start.7 = (bf16[128,3072]{1,0:T(8,128)(2,1)S(1)}, bf16[128,3072]{1,0:T(8,128)(2,1)}, u32[]{:S(2)}) copy-start(bf16[128,3072]{1,0:T(8,128)(2,1)} %gather_fusion.6) | copy-start | bytes 2359300
  231.7 2.9 %copy-start.8 = (bf16[128,3072]{1,0:T(8,128)(2,1)S(1)}, bf16[128,3072]{1,0:T(8,128)(2,1)}, u32[]{:S(2)}) copy-start(bf16[128,3072]{1,0:T(8,128)(2,1)} %gather_fusion.7) | copy-start | bytes 2359300
Sparse Core Ops, SparseCore 0:
  9.8 59.5 all-gather.1
Sparse Core Ops, SparseCore 1:
  79.2 35.2 reduce-scatter.4
  116.7 23.8 reduce-scatter.2
